TPU v7x, 256 devices: a whole 4x4x8 slice. The times are simulated.
256 devices in a mesh: gx: 4 (over y_hi, core), gy: 8 (over z), gz: 8 (over x, y_lo).
Axes of the slice: x: 4, y: 4 (y_hi: 2, y_lo: 2; y = y_hi * 2 + y_lo), z: 8, core: 2. Of those that a mesh axis runs over, the one named last changes fastest.
Arguments:
- w_minus: bfloat16 [4, 8, 8, 3, 512, 1024], P('gx', 'gy', 'gz'), may hold values from -0.25 to 0.25
- w_plus: bfloat16 [4, 8, 8, 3, 512, 1024], P('gx', 'gy', 'gz'), may hold values from -0.25 to 0.25
- interior: bfloat16 [4, 8, 8, 512, 512], P('gx', 'gy', 'gz')
- b_minus: bfloat16 [4, 8, 8, 3, 1024], P('gx', 'gy', 'gz'), may hold values from 2 to 4
- b_plus: bfloat16 [4, 8, 8, 3, 1024], P('gx', 'gy', 'gz'), may hold values from 2 to 4
- walls: int32 [4, 8, 8, 3], P('gx', 'gy', 'gz'), may hold values from 0 to 1, as said below
Outputs:
- assembled: bfloat16 [4, 8, 8, 3, 1024, 1024], P('gx', 'gy', 'gz')
Inputs may be any that keep to these rules, and one draw needn't show every extreme that they name: Every subdomain with the last index along axis a has walls 1 for axis a.
All inputs are finite; a program needn't handle non-finite values.
Results may differ from a plain program's by a relative error of at most 0.0039.
Values may be sent and summed in bfloat16 or wider, within the bound.
A program may use at most 128 MiB of HBM per device.

v0:
```python
import jax
import jax.numpy as jnp
from jax import lax
from jax.sharding import PartitionSpec as P

FSIDE = 32


def passed_along(array, axis, by):
    peers = lax.axis_size(axis)
    pairs = [(i, i + by) for i in range(peers) if 0 <= i + by < peers]
    return lax.ppermute(array, axis, pairs)


def face_links(count, side):
    cells = jnp.arange(count, dtype=jnp.int32)
    rows_u = cells // side
    rows_v = cells % side
    apart = jnp.abs(rows_u[:, None] - rows_u[None, :]) + jnp.abs(rows_v[:, None] - rows_v[None, :])
    return (apart == 1).astype(jnp.float32)


def schur_block(factor, inverse, diag_part, links):
    mapped = jnp.dot(inverse, factor, preferred_element_type=jnp.float32).astype(jnp.bfloat16)
    gram = lax.dot_general(
        factor, mapped, (((0,), (0,)), ((), ())), preferred_element_type=jnp.float32
    )
    return jnp.diag(diag_part.astype(jnp.float32)) - 0.25 * links - gram


def send_factor(factor, inverse, diag_part, axis_id):
    if axis_id == 0:
        return passed_along((factor, inverse, diag_part), "gx", -1)
    if axis_id == 1:
        return passed_along((factor, inverse, diag_part), "gy", -1)
    return passed_along((factor, inverse, diag_part), "gz", -1)


def shards(w_minus, w_plus, interior, b_minus, b_plus, walls):
    width = w_plus.shape[5]
    links = face_links(width, FSIDE)
    inverse = interior[0, 0, 0]
    blocks = []
    for axis_id in range(3):
        factor, far_inverse, diag_part = send_factor(
            w_minus[0, 0, 0, axis_id], inverse, b_minus[0, 0, 0, axis_id], axis_id
        )
        other = schur_block(factor, far_inverse, diag_part, links)
        own = schur_block(w_plus[0, 0, 0, axis_id], inverse, b_plus[0, 0, 0, axis_id], links)
        opened = walls[0, 0, 0, axis_id] == 0
        total = own + jnp.where(opened, other, jnp.zeros_like(other))
        blocks.append(total.astype(jnp.bfloat16))
    return jnp.stack(blocks)[None, None, None]


def solution(mesh):
    in_specs = (
        P("gx", "gy", "gz", None, None, None),
        P("gx", "gy", "gz", None, None, None),
        P("gx", "gy", "gz", None, None),
        P("gx", "gy", "gz", None, None),
        P("gx", "gy", "gz", None, None),
        P("gx", "gy", "gz", None),
    )
    out_specs = P("gx", "gy", "gz", None, None, None)
    return jax.shard_map(shards, mesh=mesh, in_specs=in_specs, out_specs=out_specs, check_vma=False)
```

profile of v0, /device:TPU:127, one launch (start us, length us, event | category | flops | bytes accessed | tf_op | source)
XLA Modules:
  0.0 104.1 jit_solution(3878761225398226445)
XLA Ops:
  0.0 0.9 slice_reduce_fusion.2
  0.9 2.6 %collective-permute-start = (bf16[1024]{0:T(1024)(128)(2,1)S(1)}, bf16[1024]{0:T(1024)(128)(2,1)S(1)}, u32[]{:S(2)}, u32[]{:S(2)}) collective-permute-start(bf16[1024]{0:T(1024)(128)(2,1)S(1)} %get-tuple-element.5), channel_id=1, source_target_pairs={{64,0},{128,64},{192,128},{65,1},{129,65},{193,129},{66,2},{130,66... | collective-permute-start | bytes 6152 | tf_op jit(solution)/shard_map/ppermute | solution.py:12
  3.4 2.4 %collective-permute-start.6 = (bf16[1024]{0:T(1024)(128)(2,1)S(1)}, bf16[1024]{0:T(1024)(128)(2,1)S(1)}, u32[]{:S(2)}, u32[]{:S(2)}) collective-permute-start(bf16[1024]{0:T(1024)(128)(2,1)S(1)} %get-tuple-element.6), channel_id=1, source_target_pairs={{1,0},{2,1},{3,2},{4,3},{5,4},{6,5},{7,6},{9,8},{10,9},{11,10},{12... | collective-permute-start | bytes 6152 | tf_op jit(solution)/shard_map/ppermute | solution.py:12
  5.8 1.9 %collective-permute-start.3 = (bf16[1024]{0:T(1024)(128)(2,1)S(1)}, bf16[1024]{0:T(1024)(128)(2,1)S(1)}, u32[]{:S(2)}, u32[]{:S(2)}) collective-permute-start(bf16[1024]{0:T(1024)(128)(2,1)S(1)} %get-tuple-element.7), channel_id=1, source_target_pairs={{8,0},{16,8},{24,16},{32,24},{40,32},{48,40},{56,48},{9,1},{17,9},... | collective-permute-start | bytes 6152 | tf_op jit(solution)/shard_map/ppermute | solution.py:12
  7.7 2.3 %collective-permute-start.1 = (bf16[512,512]{1,0:T(8,128)(2,1)}, bf16[512,512]{1,0:T(8,128)(2,1)S(1)}, u32[]{:S(2)}, u32[]{:S(2)}) collective-permute-start(bf16[512,512]{1,0:T(8,128)(2,1)} %bitcast.1), channel_id=1, source_target_pairs={{64,0},{128,64},{192,128},{65,1},{129,65},{193,129},{66,2},{130,66... | collective-permute-start | bytes 1572872 | tf_op jit(solution)/shard_map/ppermute | solution.py:12
  10.1 3.4 %slice_bitcast_fusion.2 = (bf16[512,1024]{1,0:T(8,128)(2,1)S(1)}, bf16[512,1024]{1,0:T(8,128)(2,1)}, bf16[512,1024]{1,0:T(8,128)(2,1)S(1)}) fusion(bf16[1,1,1,3,512,1024]{5,4,3,2,1,0:T(8,128)(2,1)} %param.6), kind=kLoop, calls=%fused_computation.43 | loop fusion | bytes 6291456 | tf_op jit(solution)/shard_map/squeeze | solution.py:46
  13.4 3.5 %collective-permute-start.2 = (bf16[512,1024]{1,0:T(8,128)(2,1)S(1)}, bf16[512,1024]{1,0:T(8,128)(2,1)}, u32[]{:S(2)}, u32[]{:S(2)}) collective-permute-start(bf16[512,1024]{1,0:T(8,128)(2,1)S(1)} %get-tuple-element.8), channel_id=1, source_target_pairs={{64,0},{128,64},{192,128},{65,1},{129,65},{193,129},{66,2},{130,66... | collective-permute-start | bytes 3145736 | tf_op jit(solution)/shard_map/ppermute | solution.py:12
  17.0 5.6 %fusion.18 = f32[1024,1024]{1,0:T(8,128)} fusion(bf16[1,1,1,3,512,1024]{5,4,3,2,1,0:T(8,128)(2,1)} %param.7, bf16[1,1,1,512,512]{4,3,2,1,0:T(8,128)(2,1)} %param.8), kind=kOutput, calls=%fused_computation.33 | convolution fusion | flops 1611137024 | bytes 6815744 | tf_op jit(solution)/shard_map/dot_general | solution.py:25
  22.5 5.5 %fusion.20 = f32[1024,1024]{1,0:T(8,128)} fusion(bf16[1,1,1,3,512,1024]{5,4,3,2,1,0:T(8,128)(2,1)} %param.7, bf16[1,1,1,512,512]{4,3,2,1,0:T(8,128)(2,1)} %param.8), kind=kOutput, calls=%fused_computation.35 | convolution fusion | flops 1611137024 | bytes 6815744 | tf_op jit(solution)/shard_map/dot_general | solution.py:25
  28.0 0.0 copy-start
  28.1 0.0 copy-start.1
  28.1 5.5 %fusion.19 = f32[1024,1024]{1,0:T(8,128)} fusion(bf16[1,1,1,3,512,1024]{5,4,3,2,1,0:T(8,128)(2,1)} %param.7, bf16[1,1,1,512,512]{4,3,2,1,0:T(8,128)(2,1)} %param.8), kind=kOutput, calls=%fused_computation.34 | convolution fusion | flops 1611137024 | bytes 6815744 | tf_op jit(solution)/shard_map/dot_general | solution.py:25
  33.5 0.0 copy-done
  33.5 0.0 collective-permute-done
  33.6 4.1 %collective-permute-start.8 = (bf16[512,1024]{1,0:T(8,128)(2,1)}, bf16[512,1024]{1,0:T(8,128)(2,1)}, u32[]{:S(2)}, u32[]{:S(2)}) collective-permute-start(bf16[512,1024]{1,0:T(8,128)(2,1)} %get-tuple-element.9), channel_id=1, source_target_pairs={{1,0},{2,1},{3,2},{4,3},{5,4},{6,5},{7,6},{9,8},{10,9},{11,10},{12... | collective-permute-start | bytes 3145736 | tf_op jit(solution)/shard_map/ppermute | solution.py:12
  37.7 0.0 copy-done.1
  37.7 0.6 fusion.46
  40.2 0.0 collective-permute-done.6
  40.3 2.2 %collective-permute-start.7 = (bf16[512,512]{1,0:T(8,128)(2,1)}, bf16[512,512]{1,0:T(8,128)(2,1)}, u32[]{:S(2)}, u32[]{:S(2)}) collective-permute-start(bf16[512,512]{1,0:T(8,128)(2,1)} %bitcast.1), channel_id=1, source_target_pairs={{1,0},{2,1},{3,2},{4,3},{5,4},{6,5},{7,6},{9,8},{10,9},{11,10},{12... | collective-permute-start | bytes 1572872 | tf_op jit(solution)/shard_map/ppermute | solution.py:12
  42.5 0.0 collective-permute-done.3
  42.5 1.9 %collective-permute-start.4 = (bf16[512,512]{1,0:T(8,128)(2,1)}, bf16[512,512]{1,0:T(8,128)(2,1)}, u32[]{:S(2)}, u32[]{:S(2)}) collective-permute-start(bf16[512,512]{1,0:T(8,128)(2,1)} %bitcast.1), channel_id=1, source_target_pairs={{8,0},{16,8},{24,16},{32,24},{40,32},{48,40},{56,48},{9,1},{17,9},... | collective-permute-start | bytes 1572872 | tf_op jit(solution)/shard_map/ppermute | solution.py:12
  44.4 0.0 collective-permute-done.1
  44.4 0.0 copy-start.2
  44.5 2.1 %collective-permute-start.5 = (bf16[512,1024]{1,0:T(8,128)(2,1)S(1)}, bf16[512,1024]{1,0:T(8,128)(2,1)}, u32[]{:S(2)}, u32[]{:S(2)}) collective-permute-start(bf16[512,1024]{1,0:T(8,128)(2,1)S(1)} %get-tuple-element.10), channel_id=1, source_target_pairs={{8,0},{16,8},{24,16},{32,24},{40,32},{48,40},{56,48},{9,1},{17,9},... | collective-permute-start | bytes 3145736 | tf_op jit(solution)/shard_map/ppermute | solution.py:12
  46.6 0.0 collective-permute-done.2
  46.6 0.0 copy-done.2
  46.6 6.8 %fusion.17 = bf16[1,1024,1024]{1,2,0:T(8,128)(2,1)S(1)} fusion(bf16[512,1024]{1,0:T(8,128)(2,1)} %collective-permute-done.2, f32[1024]{0:T(1024)S(1)} %convert_element_type.70, pred[]{:T(512)} %bitcast.4, f32[1024,1024]{1,0:T(8,128)} %fusion.18, s32[1024]{0:T(1024)S(1)} %get-tuple-element.17, s32[1024]{0:T(1024)S(1)} %get-tuple-element.18, ...), kind=kOutput, calls=%fused_computation.26 | convolution fusion | flops 1628962816 | bytes 7880705 | tf_op jit(solution)/shard_map/dot_general | solution.py:25
  53.4 17.4 %collective-permute-done.7 = bf16[512,512]{1,0:T(8,128)(2,1)} collective-permute-done((bf16[512,512]{1,0:T(8,128)(2,1)}, bf16[512,512]{1,0:T(8,128)(2,1)}, u32[]{:S(2)}, u32[]{:S(2)}) %collective-permute-start.7) | collective-permute-done | bytes 524320 | tf_op jit(solution)/shard_map/ppermute | solution.py:12
  70.8 0.0 collective-permute-done.8
  70.8 7.8 %fusion.15 = bf16[1,1024,1024]{1,2,0:T(8,128)(2,1)} fusion(bf16[512,1024]{1,0:T(8,128)(2,1)} %collective-permute-done.8, f32[1024]{0:T(1024)S(1)} %convert_element_type.82, pred[]{:T(512)} %bitcast.18, f32[1024,1024]{1,0:T(8,128)} %fusion.20, s32[1024]{0:T(1024)S(1)} %get-tuple-element.17, s32[1024]{0:T(1024)S(1)} %get-tuple-element.18, ...), kind=kOutput, calls=%fused_computation.24 | convolution fusion | flops 1628962816 | bytes 7880705 | tf_op jit(solution)/shard_map/dot_general | solution.py:25
  78.5 0.0 collective-permute-done.4
  78.5 3.7 %collective-permute-done.5 = bf16[512,1024]{1,0:T(8,128)(2,1)} collective-permute-done((bf16[512,1024]{1,0:T(8,128)(2,1)S(1)}, bf16[512,1024]{1,0:T(8,128)(2,1)}, u32[]{:S(2)}, u32[]{:S(2)}) %collective-permute-start.5) | collective-permute-done | bytes 1048608 | tf_op jit(solution)/shard_map/ppermute | solution.py:12
  82.3 7.8 %fusion.16 = bf16[1,1024,1024]{1,2,0:T(8,128)(2,1)} fusion(bf16[512,1024]{1,0:T(8,128)(2,1)} %collective-permute-done.5, f32[1024]{0:T(1024)S(1)} %convert_element_type.76, pred[]{:T(512)} %bitcast.11, f32[1024,1024]{1,0:T(8,128)} %fusion.19, s32[1024]{0:T(1024)S(1)} %get-tuple-element.17, s32[1024]{0:T(1024)S(1)} %get-tuple-element.18, ...), kind=kOutput, calls=%fused_computation.25 | convolution fusion | flops 1628962816 | bytes 7880705 | tf_op jit(solution)/shard_map/dot_general | solution.py:25
  90.1 5.5 %maximum_bitcast_fusion = bf16[1,1,1,3,1024,1024]{4,5,3,2,1,0:T(8,128)(2,1)} fusion(bf16[1,1024,1024]{1,2,0:T(8,128)(2,1)} %fusion.15, bf16[1,1024,1024]{1,2,0:T(8,128)(2,1)} %fusion.16, bf16[1,1024,1024]{1,2,0:T(8,128)(2,1)S(1)} %fusion.17), kind=kLoop, calls=%fused_computation.6 | loop fusion | flops 6291456 | bytes 12582912 | tf_op jit(solution)/shard_map/broadcast_in_dim | solution.py:53
  95.5 8.6 %copy.7 = bf16[1,1,1,3,1024,1024]{5,4,3,2,1,0:T(8,128)(2,1)} copy(bf16[1,1,1,3,1024,1024]{4,5,3,2,1,0:T(8,128)(2,1)} %maximum_bitcast_fusion) | data formatting | bytes 12582912 | tf_op jit(solution)/shard_map/broadcast_in_dim | solution.py:53
  (5 shorter events, 0.0 us)
Async XLA Ops:
  0.9 32.7 %collective-permute-start = (bf16[1024]{0:T(1024)(128)(2,1)S(1)}, bf16[1024]{0:T(1024)(128)(2,1)S(1)}, u32[]{:S(2)}, u32[]{:S(2)}) collective-permute-start(bf16[1024]{0:T(1024)(128)(2,1)S(1)} %get-tuple-element.5), channel_id=1, source_target_pairs={{64,0},{128,64},{192,128},{65,1},{129,65},{193,129},{66,2},{130,66... | collective-permute-start | bytes 6152 | tf_op jit(solution)/shard_map/ppermute | solution.py:12
  3.4 36.8 %collective-permute-start.6 = (bf16[1024]{0:T(1024)(128)(2,1)S(1)}, bf16[1024]{0:T(1024)(128)(2,1)S(1)}, u32[]{:S(2)}, u32[]{:S(2)}) collective-permute-start(bf16[1024]{0:T(1024)(128)(2,1)S(1)} %get-tuple-element.6), channel_id=1, source_target_pairs={{1,0},{2,1},{3,2},{4,3},{5,4},{6,5},{7,6},{9,8},{10,9},{11,10},{12... | collective-permute-start | bytes 6152 | tf_op jit(solution)/shard_map/ppermute | solution.py:12
  5.8 36.7 %collective-permute-start.3 = (bf16[1024]{0:T(1024)(128)(2,1)S(1)}, bf16[1024]{0:T(1024)(128)(2,1)S(1)}, u32[]{:S(2)}, u32[]{:S(2)}) collective-permute-start(bf16[1024]{0:T(1024)(128)(2,1)S(1)} %get-tuple-element.7), channel_id=1, source_target_pairs={{8,0},{16,8},{24,16},{32,24},{40,32},{48,40},{56,48},{9,1},{17,9},... | collective-permute-start | bytes 6152 | tf_op jit(solution)/shard_map/ppermute | solution.py:12
  7.7 36.7 %collective-permute-start.1 = (bf16[512,512]{1,0:T(8,128)(2,1)}, bf16[512,512]{1,0:T(8,128)(2,1)S(1)}, u32[]{:S(2)}, u32[]{:S(2)}) collective-permute-start(bf16[512,512]{1,0:T(8,128)(2,1)} %bitcast.1), channel_id=1, source_target_pairs={{64,0},{128,64},{192,128},{65,1},{129,65},{193,129},{66,2},{130,66... | collective-permute-start | bytes 1572872 | tf_op jit(solution)/shard_map/ppermute | solution.py:12
  13.4 33.1 %collective-permute-start.2 = (bf16[512,1024]{1,0:T(8,128)(2,1)S(1)}, bf16[512,1024]{1,0:T(8,128)(2,1)}, u32[]{:S(2)}, u32[]{:S(2)}) collective-permute-start(bf16[512,1024]{1,0:T(8,128)(2,1)S(1)} %get-tuple-element.8), channel_id=1, source_target_pairs={{64,0},{128,64},{192,128},{65,1},{129,65},{193,129},{66,2},{130,66... | collective-permute-start | bytes 3145736 | tf_op jit(solution)/shard_map/ppermute | solution.py:12
  28.0 5.5 %copy-start = (bf16[1,1,1,3,1024]{4,3,2,1,0:T(4,128)(2,1)S(1)}, bf16[1,1,1,3,1024]{4,3,2,1,0:T(4,128)(2,1)}, u32[]{:S(2)}) copy-start(bf16[1,1,1,3,1024]{4,3,2,1,0:T(4,128)(2,1)} %param.10) | copy-start | bytes 18436
  28.1 9.7 %copy-start.1 = (s32[1,1,1,3]{3,2,1,0:T(1,128)S(1)}, s32[1,1,1,3]{3,2,1,0:T(1,128)}, u32[]{:S(2)}) copy-start(s32[1,1,1,3]{3,2,1,0:T(1,128)} %param.11) | copy-start | bytes 40
  33.6 37.2 %collective-permute-start.8 = (bf16[512,1024]{1,0:T(8,128)(2,1)}, bf16[512,1024]{1,0:T(8,128)(2,1)}, u32[]{:S(2)}, u32[]{:S(2)}) collective-permute-start(bf16[512,1024]{1,0:T(8,128)(2,1)} %get-tuple-element.9), channel_id=1, source_target_pairs={{1,0},{2,1},{3,2},{4,3},{5,4},{6,5},{7,6},{9,8},{10,9},{11,10},{12... | collective-permute-start | bytes 3145736 | tf_op jit(solution)/shard_map/ppermute | solution.py:12
  40.3 30.5 %collective-permute-start.7 = (bf16[512,512]{1,0:T(8,128)(2,1)}, bf16[512,512]{1,0:T(8,128)(2,1)}, u32[]{:S(2)}, u32[]{:S(2)}) collective-permute-start(bf16[512,512]{1,0:T(8,128)(2,1)} %bitcast.1), channel_id=1, source_target_pairs={{1,0},{2,1},{3,2},{4,3},{5,4},{6,5},{7,6},{9,8},{10,9},{11,10},{12... | collective-permute-start | bytes 1572872 | tf_op jit(solution)/shard_map/ppermute | solution.py:12
  42.5 36.0 %collective-permute-start.4 = (bf16[512,512]{1,0:T(8,128)(2,1)}, bf16[512,512]{1,0:T(8,128)(2,1)}, u32[]{:S(2)}, u32[]{:S(2)}) collective-permute-start(bf16[512,512]{1,0:T(8,128)(2,1)} %bitcast.1), channel_id=1, source_target_pairs={{8,0},{16,8},{24,16},{32,24},{40,32},{48,40},{56,48},{9,1},{17,9},... | collective-permute-start | bytes 1572872 | tf_op jit(solution)/shard_map/ppermute | solution.py:12
  44.4 2.1 %copy-start.2 = (bf16[512,512]{1,0:T(8,128)(2,1)}, bf16[512,512]{1,0:T(8,128)(2,1)S(1)}, u32[]{:S(2)}) copy-start(bf16[512,512]{1,0:T(8,128)(2,1)S(1)} %collective-permute-done.1) | copy-start | bytes 1572868
  44.5 37.8 %collective-permute-start.5 = (bf16[512,1024]{1,0:T(8,128)(2,1)S(1)}, bf16[512,1024]{1,0:T(8,128)(2,1)}, u32[]{:S(2)}, u32[]{:S(2)}) collective-permute-start(bf16[512,1024]{1,0:T(8,128)(2,1)S(1)} %get-tuple-element.10), channel_id=1, source_target_pairs={{8,0},{16,8},{24,16},{32,24},{40,32},{48,40},{56,48},{9,1},{17,9},... | collective-permute-start | bytes 3145736 | tf_op jit(solution)/shard_map/ppermute | solution.py:12
where the time goes:
time: 105 us; the launch traced here: 104 us
  matrix products  38.9 us (37%)
  starting transfers between devices  23.1 us (22%)
  waiting for transfers between devices  21.1 us (20%)
  local copies, waits for them, and re-layouts  13.5 us (13%)
  other arithmetic  5.48 us (5%)
  between operations  2.03 us (2%)
    dot_general x6, matrix products, schur_block(): lax.dot_general(factor, mapped, (((0,), (0,)), ((), ())), preferred_eleme...  38.9 us
    ppermute x9, starting transfers between devices, passed_along(): return lax.ppermute(array, axis, pairs)  23.1 us
    ppermute x9, waiting for transfers between devices, passed_along(): return lax.ppermute(array, axis, pairs)  21.1 us
    broadcast_in_dim x1, local copies, waits for them, and re-layouts, shards(): return jnp.stack(blocks)[None, None, None]  8.61 us
    broadcast_in_dim x1, other arithmetic, shards(): return jnp.stack(blocks)[None, None, None]  5.45 us
    squeeze x1, local copies, waits for them, and re-layouts, shards(): w_minus[0, 0, 0, axis_id]  3.35 us
  transfers between devices with their start and end apart: 9, of which 2 were waited for; matrix products, arithmetic and copies ran while one was open for 34% of the time, Pallas kernels for 0%

commit v1 on v0

v1 whole, which is shorter than its diff:
```python
import jax
import jax.numpy as jnp
from jax import lax
from jax.experimental import pallas as pl
from jax.experimental.pallas import tpu as pltpu
from jax.sharding import PartitionSpec as P

FSIDE = 32
MESH = pl.DeviceIdType.MESH
PIECES = 4


def coordinates():
    gx, gy, gz = lax.axis_index("gx"), lax.axis_index("gy"), lax.axis_index("gz")
    return gz // 2, (gx // 2) * 2 + gz % 2, gy, gx % 2


def device_at(x, y, z, c):
    return ((y // 2) * 2 + c, z, x * 2 + y % 2)


def as_int(flag):
    return jnp.where(flag, 1, 0)


def kernel(
    wm_ref, wp_ref, a_ref, bm_ref, bp_ref, walls_ref, out_ref,
    wv, av, bv, bpv, walls, acc, mapped, turned, relay_a, relay_w,
    load_sem, send_sem, recv_sem, relay_send, relay_recv, forward_send,
):
    x, y, z, c = coordinates()
    rank, width = wm_ref.shape[1], wm_ref.shape[2]
    step = width // PIECES
    odd = y % 2 == 1
    even = y % 2 == 0
    low, high = y < 2, y >= 2
    c0, c1 = c == 0, c == 1

    def cols(n):
        return pl.ds(n * step, step)

    loads = [pltpu.make_async_copy(walls_ref, walls, load_sem.at[5])]
    loads.append(pltpu.make_async_copy(bp_ref, bpv, load_sem.at[4]))
    loads.append(pltpu.make_async_copy(a_ref, av.at[0], load_sem.at[3]))
    for axis in range(3):
        loads.append(pltpu.make_async_copy(wp_ref.at[axis], wv.at[axis], load_sem.at[axis]))

    has_y = z < 7
    has_z = jnp.logical_not(odd & (x == 3))
    has_x = c0 | low
    diag = even & (x >= 1)
    diag_in = odd & (x <= 2)
    relay_in = odd & ((x >= 1) | (c0 & high))
    relay_out = even & ((x >= 1) | (c0 & high))

    barrier = pltpu.get_barrier_semaphore()

    def greet(flag, *who):
        @pl.when(flag)
        def _():
            pl.semaphore_signal(barrier, inc=1, device_id=device_at(*who), device_id_type=MESH)

    greet(has_y, x, y, z + 1, c)
    greet(even, x, y + 1, z, c)
    greet(diag_in, x + 1, y - 1, z, c)
    greet(diag_in, x + 1, y, z, c)
    greet(relay_in, x, y - 1, z, c)
    greet(c0, x, y, z, 1)
    greet(c1 & low, x, y + 2, z, 0)
    greet(c1 & low, x, 1 - y, z, 0)
    greet(c1 & low, x, 3 - y, z, 0)
    greet(c0 & low, x, 3 - y, z, 0)

    for load in loads:
        load.start()

    partners = (
        as_int(z >= 1) + as_int(odd) + as_int(diag) + as_int(odd & (x >= 1)) + as_int(relay_out)
        + as_int(c1) + as_int(c0 & high) * 2 + as_int(c0)
    )
    pl.semaphore_wait(barrier, partners)

    def source(axis, part):
        if part == 0:
            return a_ref
        if part == 5:
            return bm_ref
        return wm_ref.at[axis, :, cols(part - 1)]

    def landing(axis, part):
        if part == 0:
            return av.at[1 + axis]
        if part == 5:
            return bv.at[axis]
        return wv.at[3 + axis, :, cols(part - 1)]

    def direct(axis, part, who):
        return pltpu.make_async_remote_copy(
            source(axis, part), landing(axis, part),
            send_sem.at[axis, part], recv_sem.at[axis, part],
            device_id=device_at(*who), device_id_type=MESH,
        )

    def to_relay(axis, part, slot, who):
        target = relay_a if part == 0 else relay_w.at[slot]
        return pltpu.make_async_remote_copy(
            source(axis, part), target,
            relay_send.at[axis, slot], relay_recv.at[axis, slot],
            device_id=device_at(*who), device_id_type=MESH,
        )

    def forward(axis, part, origin, slot, who):
        return pltpu.make_async_remote_copy(
            origin, landing(axis, part),
            forward_send.at[axis, slot], recv_sem.at[axis, part],
            device_id=device_at(*who), device_id_type=MESH,
        )

    y_to = (x, y, z - 1, c)
    z_to_even = (x, y - 1, z, c)
    z_to_odd = (x - 1, y + 1, z, c)
    side = (x, y + 1, z, c)
    x_near = (x, y, z, 0)
    x_far = (x, y - 2, z, 1)
    x_relay = (x, 3 - y, z, 0)

    sent = []

    def send(flag, copy):
        @pl.when(flag)
        def _():
            copy.start()

        sent.append((flag, copy))

    send(z >= 1, direct(1, 5, y_to))
    send(odd, direct(2, 5, z_to_even))
    send(diag, direct(2, 5, z_to_odd))
    send(c1, direct(0, 5, x_near))
    send(c0 & high, direct(0, 5, x_far))
    send(relay_out, to_relay(2, 0, 3, side))
    send(diag & (x >= 2), to_relay(2, 1, 0, side))
    send(diag & (x >= 3), to_relay(2, 2, 1, side))
    send(c0 & high, to_relay(0, 1, 2, x_relay))
    send(c0 & (y == 3), to_relay(0, 2, 0, x_relay))
    send(c0 & (y == 3), to_relay(0, 3, 1, x_relay))
    for part in range(5):
        send(z >= 1, direct(1, part, y_to))
        send(odd, direct(2, part, z_to_even))
        send(c1, direct(0, part, x_near))
        if part == 1:
            send(diag & (x < 2), direct(2, part, z_to_odd))
        elif part == 2:
            send(diag & (x < 3), direct(2, part, z_to_odd))
        elif part > 2:
            send(diag, direct(2, part, z_to_odd))
        if part == 4:
            send(c0 & high, direct(0, part, x_far))
        elif part > 1:
            send(c0 & (y == 2), direct(0, part, x_far))

    forwarded = []

    def pass_on(flag, arrival, copies):
        @pl.when(flag)
        def _():
            arrival.wait_recv()
            for when, copy in copies:
                if when is None:
                    copy.start()
                else:
                    pl.when(when)(copy.start)

        for when, copy in copies:
            forwarded.append((flag if when is None else flag & when, copy))

    def x_relays():
        target = (x, 1 - y, z, 1)
        for part, slot in ((1, 2), (2, 0), (3, 1)):
            pass_on(
                (c0 & low) if part == 1 else (c0 & (y == 0)), to_relay(0, part, slot, x_relay),
                [(None, forward(0, part, relay_w.at[slot], slot, target))],
            )

    def interior_relay():
        pass_on(
            relay_in, to_relay(2, 0, 3, side),
            [
                (x >= 1, forward(2, 0, relay_a, 3, (x - 1, y, z, c))),
                (c0 & high, forward(0, 0, relay_a, 3, (x, y - 3, z, 1))),
            ],
        )

    def near_interior():
        pass_on(
            c0 & (y == 2), direct(2, 0, z_to_even),
            [(None, forward(0, 0, av.at[3], 3, (x, 1, z, 1)))],
        )

    def piece_relay(part):
        slot = part - 1
        pass_on(
            odd & (x >= part + 1), to_relay(2, part, slot, side),
            [(None, forward(2, part, relay_w.at[slot], slot, (x - 1, y, z, c)))],
        )

    def open_face(axis):
        return walls[axis] == 0

    def map_piece(w, a, m, n):
        piece = wv[w, :, cols(n)]
        mapped[m, :, cols(n)] = jnp.dot(
            av[a], piece, preferred_element_type=jnp.float32
        ).astype(jnp.bfloat16)
        turned[m, cols(n), :] = piece.T

    def upper(axis, carry):
        @pl.when(axis == 0)
        def _():
            loads[2].wait()

        pltpu.make_async_copy(wp_ref.at[axis], wv.at[axis], load_sem.at[axis]).wait()
        for n in range(PIECES):
            map_piece(axis, 0, axis, n)
        for n in range(PIECES):
            acc[axis, cols(n), :] = -jnp.dot(
                turned[axis, cols(n), :], mapped[axis], preferred_element_type=jnp.float32
            )
        return carry

    def edges(axis):
        band = step // 2
        is_open = open_face(axis)
        own = bpv[axis : axis + 1, :].astype(jnp.float32)
        other = bv[axis, axis : axis + 1, :].astype(jnp.float32)
        total = own + jnp.where(is_open, other, 0.0)
        link = jnp.where(is_open, -0.5, -0.25)

        def one(n, carry):
            shape = (band, width)
            p = lax.broadcasted_iota(jnp.int32, shape, 0) + n * band
            q = lax.broadcasted_iota(jnp.int32, shape, 1)
            apart = jnp.abs((p >> 5) - (q >> 5)) + jnp.abs((p & 31) - (q & 31))
            base = jnp.where(p == q, total, jnp.where(apart == 1, link, 0.0))
            rows = pl.ds(pl.multiple_of(n * band, band), band)
            acc[axis, rows, :] += base
            return carry

        lax.fori_loop(0, width // band, one, 0)

    def finish(axis, rows, columns, gram):
        total = acc[axis, rows, columns] - jnp.where(open_face(axis), gram, 0.0)
        out_ref[axis, rows, columns] = total.astype(jnp.bfloat16)

    def lower(axis, n):
        map_piece(3 + axis, 1 + axis, axis, n)
        seen = pl.ds(0, (n + 1) * step)
        finish(axis, cols(n), seen, jnp.dot(
            turned[axis, cols(n), :], mapped[axis, :, seen], preferred_element_type=jnp.float32
        ))
        if n:
            before = pl.ds(0, n * step)
            finish(axis, before, cols(n), jnp.dot(
                turned[axis, before, :], mapped[axis, :, cols(n)],
                preferred_element_type=jnp.float32,
            ))

    def arrived(axis, part):
        if part == 0:
            target = av.at[1 + axis]
        elif part == 5:
            target = bv.at[axis]
        else:
            target = wv.at[3 + axis, :, cols(part - 1)]
        source_ref = a_ref if part == 0 else bm_ref if part == 5 else wm_ref.at[axis, :, cols(part - 1)]
        pltpu.make_async_remote_copy(
            source_ref, target, send_sem.at[axis, part], recv_sem.at[axis, part],
            device_id=device_at(x, y, z, 1 - c), device_id_type=MESH,
        ).wait_recv()

    def wait_part(axis, part):
        if axis == 2 and part == 0:
            pl.when(has_z & jnp.logical_not(c0 & (y == 2)))(lambda: arrived(axis, part))
        else:
            pl.when((has_x, has_y, has_z)[axis])(lambda: arrived(axis, part))

    x_relays()
    lax.fori_loop(0, 3, upper, 0)
    near_interior()
    loads[0].wait()
    loads[1].wait()
    for axis in range(3):
        wait_part(axis, 5)
    for axis in range(3):
        edges(axis)

    @pl.when(c0)
    def _():
        arrived(0, 0)
        for n in range(PIECES):
            arrived(0, n + 1)
            lower(0, n)

    late_x = c1 & low

    def plain(axis, flag):
        @pl.when(flag)
        def _():
            out_ref[axis] = acc[axis].astype(jnp.bfloat16)

    plain(0, c1 & high)
    plain(1, jnp.logical_not(has_y))
    plain(2, jnp.logical_not(has_z))

    interior_relay()
    piece_relay(1)
    piece_relay(2)

    wait_part(1, 0)
    wait_part(2, 0)

    @pl.when(late_x)
    def _():
        arrived(0, 0)

    for n in range(PIECES):
        def one(t, carry, n=n):
            axis = (t + 1) % 3
            flag = ((axis == 0) & late_x) | ((axis == 1) & has_y) | ((axis == 2) & has_z)

            @pl.when(flag)
            def _():
                arrived(axis, n + 1)
                lower(axis, n)

            return carry

        lax.fori_loop(0, 3, one, 0)

    for flag, copy in sent + forwarded:
        pl.when(flag)(copy.wait_send)


def shards(w_minus, w_plus, interior, b_minus, b_plus, walls):
    rank, width = w_plus.shape[4:]
    faces = 3
    step = width // PIECES
    any_spec = pl.BlockSpec(memory_space=pltpu.HBM)
    out = pl.pallas_call(
        kernel,
        out_shape=pltpu.VMEM((faces, width, width), jnp.bfloat16),
        in_specs=[any_spec] * 6,
        out_specs=pl.BlockSpec(memory_space=pltpu.VMEM),
        scratch_shapes=[
            pltpu.VMEM((6, rank, width), jnp.bfloat16),
            pltpu.VMEM((4, rank, rank), jnp.bfloat16),
            pltpu.VMEM((3, faces, width), jnp.bfloat16),
            pltpu.VMEM((faces, width), jnp.bfloat16),
            pltpu.SMEM((faces,), jnp.int32),
            pltpu.VMEM((faces, width, width), jnp.float32),
            pltpu.VMEM((faces, rank, width), jnp.bfloat16),
            pltpu.VMEM((faces, width, rank), jnp.bfloat16),
            pltpu.VMEM((rank, rank), jnp.bfloat16),
            pltpu.VMEM((3, rank, step), jnp.bfloat16),
            pltpu.SemaphoreType.DMA((6,)),
            pltpu.SemaphoreType.DMA((3, 6)),
            pltpu.SemaphoreType.DMA((3, 6)),
            pltpu.SemaphoreType.DMA((3, 4)),
            pltpu.SemaphoreType.DMA((3, 4)),
            pltpu.SemaphoreType.DMA((3, 4)),
        ],
        compiler_params=pltpu.CompilerParams(
            collective_id=0, has_side_effects=True, vmem_limit_bytes=60000000
        ),
    )(
        w_minus[0, 0, 0], w_plus[0, 0, 0], interior[0, 0, 0], b_minus[0, 0, 0], b_plus[0, 0, 0],
        walls[0, 0, 0],
    )
    return out[None, None, None]


def solution(mesh):
    in_specs = (
        P("gx", "gy", "gz", None, None, None),
        P("gx", "gy", "gz", None, None, None),
        P("gx", "gy", "gz", None, None),
        P("gx", "gy", "gz", None, None),
        P("gx", "gy", "gz", None, None),
        P("gx", "gy", "gz", None),
    )
    out_specs = P("gx", "gy", "gz", None, None, None)
    return jax.shard_map(shards, mesh=mesh, in_specs=in_specs, out_specs=out_specs, check_vma=False)
```

time: 105 us -> 61.2 us (0.58)
  the two profiles are of different devices: /device:TPU:127 before, /device:TPU:1 now
where the time goes in v1:
time: 61.2 us
  Pallas kernels  58.5 us (96%)
  local copies, waits for them, and re-layouts  2.71 us (4%)
    pallas_call x1, Pallas kernels, shards(): pl.pallas_call(kernel, out_shape=pltpu.VMEM((faces, width, width), jnp.bf...  58.5 us
    unnamed x1, local copies, waits for them, and re-layouts  2.71 us

profile of v1, /device:TPU:1, one launch (start us, length us, event | category | flops | bytes accessed | tf_op | source)
XLA Modules:
  0.0 61.2 jit_solution(1938286930517947660)
XLA Ops:
  0.0 58.5 %shard_map.64 = bf16[3,1024,1024]{2,1,0:T(8,128)(2,1)S(1)} custom-call(bf16[3,512,1024]{2,1,0:T(8,128)(2,1)} %bitcast.8, bf16[3,512,1024]{2,1,0:T(8,128)(2,1)} %bitcast.9, bf16[512,512]{1,0:T(8,128)(2,1)} %bitcast.10, bf16[3,1024]{1,0:T(4,128)(2,1)} %bitcast.11, bf16[3,1024]{1,0:T(4,128)(2,1)} %bitcast.12, s32[3]{0:T(128)} %bitcast.13), custom_call_target="tpu_custom_call" | custom-call | tf_op jit(solution)/shard_map/pallas_call | solution.py:349
  58.5 2.7 %copy.8 = bf16[1,1,1,3,1024,1024]{5,4,3,2,1,0:T(8,128)(2,1)} copy(bf16[1,1,1,3,1024,1024]{5,4,3,2,1,0:T(8,128)(2,1)S(1)} %bitcast.7) | data formatting | bytes 12582912

commit v2 on v1

--- a/solution.py
+++ b/solution.py
@@ -25,7 +25,7 @@
 
 def kernel(
     wm_ref, wp_ref, a_ref, bm_ref, bp_ref, walls_ref, out_ref,
-    wv, av, bv, bpv, walls, acc, mapped, turned, relay_a, relay_w,
+    wv, av, bv, bpv, walls, lows, acc, mapped, turned, relay_a, relay_w,
     load_sem, send_sem, recv_sem, relay_send, relay_recv, forward_send,
 ):
     x, y, z, c = coordinates()
@@ -39,11 +39,15 @@
     def cols(n):
         return pl.ds(n * step, step)
 
+    to_send = [pltpu.make_async_copy(a_ref, av.at[0], load_sem.at[3])]
+    for axis in (2, 0):
+        to_send.append(pltpu.make_async_copy(wm_ref.at[axis], lows.at[axis], load_sem.at[6 + axis]))
     loads = [pltpu.make_async_copy(walls_ref, walls, load_sem.at[5])]
     loads.append(pltpu.make_async_copy(bp_ref, bpv, load_sem.at[4]))
-    loads.append(pltpu.make_async_copy(a_ref, av.at[0], load_sem.at[3]))
     for axis in range(3):
         loads.append(pltpu.make_async_copy(wp_ref.at[axis], wv.at[axis], load_sem.at[axis]))
+    for load in to_send + loads:
+        load.start()
 
     has_y = z < 7
     has_z = jnp.logical_not(odd & (x == 3))
@@ -71,28 +75,35 @@
     greet(c1 & low, x, 3 - y, z, 0)
     greet(c0 & low, x, 3 - y, z, 0)
 
-    for load in loads:
-        load.start()
-
     partners = (
         as_int(z >= 1) + as_int(odd) + as_int(diag) + as_int(odd & (x >= 1)) + as_int(relay_out)
         + as_int(c1) + as_int(c0 & high) * 2 + as_int(c0)
     )
     pl.semaphore_wait(barrier, partners)
 
+    half = rank // 2
+
+    def halves(part):
+        return pl.ds(part * half, half)
+
     def source(axis, part):
-        if part == 0:
-            return a_ref
-        if part == 5:
+        if part < 2:
+            return a_ref.at[halves(part)]
+        if part == 6:
             return bm_ref
-        return wm_ref.at[axis, :, cols(part - 1)]
+        if axis == 1:
+            return wm_ref.at[axis, :, cols(part - 2)]
+        return lows.at[axis, :, cols(part - 2)]
 
     def landing(axis, part):
-        if part == 0:
-            return av.at[1 + axis]
-        if part == 5:
+        if part < 2:
+            return av.at[1 + axis, halves(part)]
+        if part == 6:
             return bv.at[axis]
-        return wv.at[3 + axis, :, cols(part - 1)]
+        return wv.at[3 + axis, :, cols(part - 2)]
+
+    def slot_ref(slot):
+        return relay_a.at[halves(slot)] if slot < 2 else relay_w.at[slot - 2]
 
     def direct(axis, part, who):
         return pltpu.make_async_remote_copy(
@@ -102,9 +113,8 @@
         )
 
     def to_relay(axis, part, slot, who):
-        target = relay_a if part == 0 else relay_w.at[slot]
         return pltpu.make_async_remote_copy(
-            source(axis, part), target,
+            source(axis, part), slot_ref(slot),
             relay_send.at[axis, slot], relay_recv.at[axis, slot],
             device_id=device_at(*who), device_id_type=MESH,
         )
@@ -133,31 +143,54 @@
 
         sent.append((flag, copy))
 
-    send(z >= 1, direct(1, 5, y_to))
-    send(odd, direct(2, 5, z_to_even))
-    send(diag, direct(2, 5, z_to_odd))
-    send(c1, direct(0, 5, x_near))
-    send(c0 & high, direct(0, 5, x_far))
-    send(relay_out, to_relay(2, 0, 3, side))
-    send(diag & (x >= 2), to_relay(2, 1, 0, side))
-    send(diag & (x >= 3), to_relay(2, 2, 1, side))
-    send(c0 & high, to_relay(0, 1, 2, x_relay))
-    send(c0 & (y == 3), to_relay(0, 2, 0, x_relay))
-    send(c0 & (y == 3), to_relay(0, 3, 1, x_relay))
-    for part in range(5):
+    send(z >= 1, direct(1, 6, y_to))
+    send(odd, direct(2, 6, z_to_even))
+    send(diag, direct(2, 6, z_to_odd))
+    send(c1, direct(0, 6, x_near))
+    send(c0 & high, direct(0, 6, x_far))
+    def goes_round(part):
+        return x + c >= part
+
+    diagonal_relayed = [
+        (relay_out, to_relay(2, 0, 0, side)),
+        (relay_out, to_relay(2, 1, 1, side)),
+        (diag & goes_round(2), to_relay(2, 2, 2, side)),
+        (diag & goes_round(3), to_relay(2, 3, 3, side)),
+        (diag & goes_round(4), to_relay(2, 4, 4, side)),
+    ]
+    for flag, copy in diagonal_relayed[:2]:
+        pl.when(flag)(copy.start)
+    for part in range(2):
+        send(odd, direct(2, part, z_to_even))
+    for part in range(6):
         send(z >= 1, direct(1, part, y_to))
-        send(odd, direct(2, part, z_to_even))
+    for load in to_send:
+        load.wait()
+    for flag, copy in diagonal_relayed[2:]:
+        pl.when(flag)(copy.start)
+    send(c0 & high, to_relay(0, 2, 5, x_relay))
+    send(c0 & (y == 3), to_relay(0, 3, 2, x_relay))
+    send(c0 & (y == 3), to_relay(0, 4, 3, x_relay))
+    send(c0 & (y == 3), direct(0, 5, x_far))
+    corner = c0 & (x == 0)
+    for part in (3, 4, 5):
+        send(c0 & (y == 2) & (x >= 1), direct(0, part, x_far))
+        send(corner & (y == 2), to_relay(0, part, part - 1, side))
+    keeps = c0 & (y == 1)
+    for part in range(2, 6):
+        send(odd & jnp.logical_not(keeps) if part > 3 else odd, direct(2, part, z_to_even))
+    for part in range(6):
         send(c1, direct(0, part, x_near))
-        if part == 1:
-            send(diag & (x < 2), direct(2, part, z_to_odd))
-        elif part == 2:
-            send(diag & (x < 3), direct(2, part, z_to_odd))
-        elif part > 2:
-            send(diag, direct(2, part, z_to_odd))
-        if part == 4:
-            send(c0 & high, direct(0, part, x_far))
-        elif part > 1:
-            send(c0 & (y == 2), direct(0, part, x_far))
+    straight = [
+        (diag & jnp.logical_not(goes_round(part)), direct(2, part, z_to_odd)) for part in range(2, 5)
+    ] + [(diag, direct(2, 5, z_to_odd))]
+    sent.extend(straight)
+
+    def send_diagonal(now):
+        for flag, copy in diagonal_relayed:
+            pl.when(flag & now)(copy.wait_send)
+        for flag, copy in straight:
+            pl.when(flag & now)(copy.start)
 
     forwarded = []
 
@@ -174,34 +207,50 @@
         for when, copy in copies:
             forwarded.append((flag if when is None else flag & when, copy))
 
-    def x_relays():
-        target = (x, 1 - y, z, 1)
-        for part, slot in ((1, 2), (2, 0), (3, 1)):
-            pass_on(
-                (c0 & low) if part == 1 else (c0 & (y == 0)), to_relay(0, part, slot, x_relay),
-                [(None, forward(0, part, relay_w.at[slot], slot, target))],
-            )
-
-    def interior_relay():
+    x_relayed = ((c0 & low, 2, 5), (c0 & (y == 0), 3, 2), (c0 & (y == 0), 4, 3))
+
+    def x_forward(part, slot):
+        return forward(0, part, slot_ref(slot), slot, (x, 1 - y, z, 1))
+
+    def x_relay_piece(n, when):
+        flag, part, slot = x_relayed[n]
+
+        @pl.when(flag & when)
+        def _():
+            to_relay(0, part, slot, x_relay).wait_recv()
+            x_forward(part, slot).start()
+
+    for flag, part, slot in x_relayed:
+        forwarded.append((flag, x_forward(part, slot)))
+
+    def interior_relay(part):
         pass_on(
-            relay_in, to_relay(2, 0, 3, side),
+            relay_in, to_relay(2, part, part, side),
             [
-                (x >= 1, forward(2, 0, relay_a, 3, (x - 1, y, z, c))),
-                (c0 & high, forward(0, 0, relay_a, 3, (x, y - 3, z, 1))),
+                (x >= 1, forward(2, part, slot_ref(part), part, (x - 1, y, z, c))),
+                (c0 & high, forward(0, part, slot_ref(part), part, (x, y - 3, z, 1))),
             ],
         )
 
+    def corner_relay():
+        for part in (3, 4, 5):
+            slot = part - 1
+            pass_on(
+                corner & (y == 3), to_relay(0, part, slot, side),
+                [(None, forward(0, part, slot_ref(slot), slot, (x, 0, z, 1)))],
+            )
+
     def near_interior():
+        for part in range(2):
+            pass_on(
+                c0 & (y == 2), direct(2, part, z_to_even),
+                [(None, forward(0, part, av.at[3, halves(part)], part, (x, 1, z, 1)))],
+            )
+
+    def piece_relay(part):
         pass_on(
-            c0 & (y == 2), direct(2, 0, z_to_even),
-            [(None, forward(0, 0, av.at[3], 3, (x, 1, z, 1)))],
-        )
-
-    def piece_relay(part):
-        slot = part - 1
-        pass_on(
-            odd & (x >= part + 1), to_relay(2, part, slot, side),
-            [(None, forward(2, part, relay_w.at[slot], slot, (x - 1, y, z, c)))],
+            odd & goes_round(part), to_relay(2, part, part, side),
+            [(None, forward(2, part, slot_ref(part), part, (x - 1, y, z, c)))],
         )
 
     def open_face(axis):
@@ -215,9 +264,6 @@
         turned[m, cols(n), :] = piece.T
 
     def upper(axis, carry):
-        @pl.when(axis == 0)
-        def _():
-            loads[2].wait()
 
         pltpu.make_async_copy(wp_ref.at[axis], wv.at[axis], load_sem.at[axis]).wait()
         for n in range(PIECES):
@@ -266,41 +312,49 @@
             ))
 
     def arrived(axis, part):
-        if part == 0:
-            target = av.at[1 + axis]
-        elif part == 5:
-            target = bv.at[axis]
-        else:
-            target = wv.at[3 + axis, :, cols(part - 1)]
-        source_ref = a_ref if part == 0 else bm_ref if part == 5 else wm_ref.at[axis, :, cols(part - 1)]
         pltpu.make_async_remote_copy(
-            source_ref, target, send_sem.at[axis, part], recv_sem.at[axis, part],
+            landing(axis, part), landing(axis, part),
+            send_sem.at[axis, part], recv_sem.at[axis, part],
             device_id=device_at(x, y, z, 1 - c), device_id_type=MESH,
         ).wait_recv()
 
     def wait_part(axis, part):
-        if axis == 2 and part == 0:
+        if axis == 2 and part < 2:
             pl.when(has_z & jnp.logical_not(c0 & (y == 2)))(lambda: arrived(axis, part))
         else:
             pl.when((has_x, has_y, has_z)[axis])(lambda: arrived(axis, part))
 
-    x_relays()
+    for n in range(2):
+        x_relay_piece(n, True)
+    for part in (4, 5):
+        send(keeps, direct(2, part, z_to_even))
+    x_relay_piece(2, x == 0)
     lax.fori_loop(0, 3, upper, 0)
+    x_relay_piece(2, x >= 1)
+    send_diagonal(c0 & (x <= 1) & (y == 0))
+    interior_relay(0)
     near_interior()
     loads[0].wait()
     loads[1].wait()
     for axis in range(3):
-        wait_part(axis, 5)
-    for axis in range(3):
-        edges(axis)
+        wait_part(axis, 6)
+    edges(0)
+    edges(1)
+    interior_relay(1)
+    edges(2)
+    send_diagonal((x <= 1) & c1)
+    send_diagonal((x == 2) & c0 & (y == 0))
 
     @pl.when(c0)
     def _():
         arrived(0, 0)
+        arrived(0, 1)
         for n in range(PIECES):
-            arrived(0, n + 1)
+            arrived(0, n + 2)
             lower(0, n)
 
+    send_diagonal((x <= 1) & c0 & (y > 0))
+    corner_relay()
     late_x = c1 & low
 
     def plain(axis, flag):
@@ -308,34 +362,50 @@
         def _():
             out_ref[axis] = acc[axis].astype(jnp.bfloat16)
 
+    piece_relay(2)
     plain(0, c1 & high)
     plain(1, jnp.logical_not(has_y))
     plain(2, jnp.logical_not(has_z))
-
-    interior_relay()
-    piece_relay(1)
-    piece_relay(2)
-
-    wait_part(1, 0)
-    wait_part(2, 0)
-
-    @pl.when(late_x)
-    def _():
-        arrived(0, 0)
-
-    for n in range(PIECES):
-        def one(t, carry, n=n):
-            axis = (t + 1) % 3
-            flag = ((axis == 0) & late_x) | ((axis == 1) & has_y) | ((axis == 2) & has_z)
-
-            @pl.when(flag)
+    piece_relay(3)
+    send_diagonal((x == 2) & (c1 | (y > 0)))
+
+    for part in range(2):
+        wait_part(1, part)
+        wait_part(2, part)
+
+    def y_and_z(n):
+        def one(t, carry):
+            axis = t + 1
+
+            @pl.when(((axis == 1) & has_y) | ((axis == 2) & has_z))
             def _():
-                arrived(axis, n + 1)
+                arrived(axis, n + 2)
                 lower(axis, n)
 
             return carry
 
-        lax.fori_loop(0, 3, one, 0)
+        lax.fori_loop(0, 2, one, 0)
+
+    y_and_z(0)
+    y_and_z(1)
+
+    def x_late(*pieces):
+        @pl.when(late_x)
+        def _():
+            for n in pieces:
+                arrived(0, n + 2)
+                lower(0, n)
+
+    for part in range(2):
+        pl.when(late_x)(lambda part=part: arrived(0, part))
+    x_late(0)
+    piece_relay(4)
+    send_diagonal(x == 3)
+    x_late(1)
+    y_and_z(2)
+    x_late(2)
+    y_and_z(3)
+    x_late(3)
 
     for flag, copy in sent + forwarded:
         pl.when(flag)(copy.wait_send)
@@ -357,17 +427,18 @@
             pltpu.VMEM((3, faces, width), jnp.bfloat16),
             pltpu.VMEM((faces, width), jnp.bfloat16),
             pltpu.SMEM((faces,), jnp.int32),
+            pltpu.VMEM((faces, rank, width), jnp.bfloat16),
             pltpu.VMEM((faces, width, width), jnp.float32),
             pltpu.VMEM((faces, rank, width), jnp.bfloat16),
             pltpu.VMEM((faces, width, rank), jnp.bfloat16),
             pltpu.VMEM((rank, rank), jnp.bfloat16),
-            pltpu.VMEM((3, rank, step), jnp.bfloat16),
-            pltpu.SemaphoreType.DMA((6,)),
+            pltpu.VMEM((PIECES, rank, step), jnp.bfloat16),
+            pltpu.SemaphoreType.DMA((9,)),
+            pltpu.SemaphoreType.DMA((3, 7)),
+            pltpu.SemaphoreType.DMA((3, 7)),
             pltpu.SemaphoreType.DMA((3, 6)),
             pltpu.SemaphoreType.DMA((3, 6)),
-            pltpu.SemaphoreType.DMA((3, 4)),
-            pltpu.SemaphoreType.DMA((3, 4)),
-            pltpu.SemaphoreType.DMA((3, 4)),
+            pltpu.SemaphoreType.DMA((3, 6)),
         ],
         compiler_params=pltpu.CompilerParams(
             collective_id=0, has_side_effects=True, vmem_limit_bytes=60000000

time: 61.2 us -> 46.5 us (0.76)
  the two profiles are of different devices: /device:TPU:1 before, /device:TPU:109 now
where the time goes in v2:
time: 46.5 us
  Pallas kernels  43.7 us (94%)
  local copies, waits for them, and re-layouts  2.71 us (6%)
    pallas_call x1, Pallas kernels, shards(): pl.pallas_call(kernel, out_shape=pltpu.VMEM((faces, width, width), jnp.bf...  43.7 us
    unnamed x1, local copies, waits for them, and re-layouts  2.71 us

profile of v2, /device:TPU:109, one launch (start us, length us, event | category | flops | bytes accessed | tf_op | source)
XLA Modules:
  0.0 46.5 jit_solution(14525597153008498361)
XLA Ops:
  0.0 43.7 %shard_map.64 = bf16[3,1024,1024]{2,1,0:T(8,128)(2,1)S(1)} custom-call(bf16[3,512,1024]{2,1,0:T(8,128)(2,1)} %bitcast.8, bf16[3,512,1024]{2,1,0:T(8,128)(2,1)} %bitcast.9, bf16[512,512]{1,0:T(8,128)(2,1)} %bitcast.10, bf16[3,1024]{1,0:T(4,128)(2,1)} %bitcast.11, bf16[3,1024]{1,0:T(4,128)(2,1)} %bitcast.12, s32[3]{0:T(128)} %bitcast.13), custom_call_target="tpu_custom_call" | custom-call | tf_op jit(solution)/shard_map/pallas_call | solution.py:419
  43.8 2.7 %copy.8 = bf16[1,1,1,3,1024,1024]{5,4,3,2,1,0:T(8,128)(2,1)} copy(bf16[1,1,1,3,1024,1024]{5,4,3,2,1,0:T(8,128)(2,1)S(1)} %bitcast.7) | data formatting | bytes 12582912

commit v3 on v2

--- a/solution.py
+++ b/solution.py
@@ -149,7 +149,7 @@
     send(c1, direct(0, 6, x_near))
     send(c0 & high, direct(0, 6, x_far))
     def goes_round(part):
-        return x + c >= part
+        return ((x != 2) & (x + c >= part)) | ((x == 2) & c1 & (part < 5))
 
     diagonal_relayed = [
         (relay_out, to_relay(2, 0, 0, side)),
@@ -387,6 +387,10 @@
         lax.fori_loop(0, 2, one, 0)
 
     y_and_z(0)
+    early = (x == 3) & c0 & (y == 2)
+    for flag, copy in diagonal_relayed:
+        pl.when(flag & early)(copy.wait_send)
+    pl.when(early)(straight[2][1].start)
     y_and_z(1)
 
     def x_late(*pieces):
@@ -400,7 +404,8 @@
         pl.when(late_x)(lambda part=part: arrived(0, part))
     x_late(0)
     piece_relay(4)
-    send_diagonal(x == 3)
+    send_diagonal((x == 3) & jnp.logical_not(early))
+    pl.when(early)(straight[3][1].start)
     x_late(1)
     y_and_z(2)
     x_late(2)

time: 46.5 us -> 46.6 us (level)
  no operation moved by 1% of the time
where the time goes in v3:
time: 46.6 us; the launch traced here: 46.5 us
  Pallas kernels  43.7 us (94%)
  local copies, waits for them, and re-layouts  2.71 us (6%)
    pallas_call x1, Pallas kernels, shards(): pl.pallas_call(kernel, out_shape=pltpu.VMEM((faces, width, width), jnp.bf...  43.7 us
    unnamed x1, local copies, waits for them, and re-layouts  2.71 us

profile of v3, /device:TPU:109, one launch (start us, length us, event | category | flops | bytes accessed | tf_op | source)
XLA Modules:
  0.0 46.5 jit_solution(18219932514201710484)
XLA Ops:
  0.0 43.7 %shard_map.64 = bf16[3,1024,1024]{2,1,0:T(8,128)(2,1)S(1)} custom-call(bf16[3,512,1024]{2,1,0:T(8,128)(2,1)} %bitcast.8, bf16[3,512,1024]{2,1,0:T(8,128)(2,1)} %bitcast.9, bf16[512,512]{1,0:T(8,128)(2,1)} %bitcast.10, bf16[3,1024]{1,0:T(4,128)(2,1)} %bitcast.11, bf16[3,1024]{1,0:T(4,128)(2,1)} %bitcast.12, s32[3]{0:T(128)} %bitcast.13), custom_call_target="tpu_custom_call" | custom-call | tf_op jit(solution)/shard_map/pallas_call | solution.py:424
  43.8 2.7 %copy.8 = bf16[1,1,1,3,1024,1024]{5,4,3,2,1,0:T(8,128)(2,1)} copy(bf16[1,1,1,3,1024,1024]{5,4,3,2,1,0:T(8,128)(2,1)S(1)} %bitcast.7) | data formatting | bytes 12582912
